TPU v7x, 32 devices: a whole 2x2x4 slice. The times are simulated.
32 devices in a mesh: node: 8 (over y, x, core), grp: 4 (over z).
Axes of the slice: x: 2, y: 2, z: 4, core: 2. Of those that a mesh axis runs over, the one named last changes fastest.
Arguments:
- tokens: bfloat16 [12288, 1792], P(('node', 'grp')), may hold values from -6 to 6
- cotangent: bfloat16 [12288, 1792], P(('node', 'grp')), may hold values from -6 to 6
- gate_weight: bfloat16 [1792, 1024], P('node'), may hold values from -0.125 to 0.125
- up_weight: bfloat16 [1792, 1024], P('node'), may hold values from -0.125 to 0.125
- down_weight_t: bfloat16 [1792, 1024], P('node'), may hold values from -0.125 to 0.125
- error_memory: bfloat16 [4, 1792, 3072], P('grp', 'node'), may hold values from -4 to 4
- q_init: float32 [3, 1024, 32], replicated, may hold values from -6 to 6
Outputs:
- token_grad: bfloat16 [12288, 1792], P(('node', 'grp'))
- new_error: bfloat16 [4, 1792, 3072], P('grp', 'node')
- p_hat: float32 [3, 1792, 32], P(None, 'node')
- q_new: float32 [3, 1024, 32], replicated
All inputs are finite; a program needn't handle non-finite values.
Results may differ from a plain program's by a relative error of at most 0.012.
Values may be sent and summed in bfloat16 or wider, within the bound.
A program may use at most 192 MiB of HBM per device.

v0:
```python
import math
import jax
import jax.numpy as jnp
from jax import lax
from jax.sharding import PartitionSpec as P


def gelu_parts(value):
    coeff = math.sqrt(2.0 / math.pi)
    inner = coeff * (value + 0.044715 * value * value * value)
    tanh_value = jnp.tanh(inner)
    activation = 0.5 * value * (1.0 + tanh_value)
    slope = 0.5 * (1.0 + tanh_value) + 0.5 * value * (1.0 - tanh_value * tanh_value) * coeff * (
        1.0 + 3.0 * 0.044715 * value * value
    )
    return (activation, slope)


def contract_rows(left_side, right_side):
    return lax.dot_general(
        left_side, right_side, (((0,), (0,)), ((), ())), preferred_element_type=jnp.float32
    )


def on_device(tokens, cotangent, gate_weight, up_weight, down_weight_t, error_memory, q_init):
    node_count = lax.axis_size("node")
    group_count = lax.axis_size("grp")
    hidden_units = gate_weight.shape[1]
    highest = lax.Precision.HIGHEST
    full_gate, full_up, full_down = (
        lax.all_gather(gate_weight, "node", axis=0, tiled=True),
        lax.all_gather(up_weight, "node", axis=0, tiled=True),
        lax.all_gather(down_weight_t, "node", axis=0, tiled=True),
    )
    gate_pre = jnp.dot(tokens, full_gate, preferred_element_type=jnp.float32)
    up_pre = jnp.dot(tokens, full_up, preferred_element_type=jnp.float32)
    activation, slope = gelu_parts(gate_pre)
    hidden = (activation * up_pre).astype(jnp.bfloat16)
    back_hidden = jnp.dot(cotangent, full_down, preferred_element_type=jnp.float32)
    grad_up = (back_hidden * activation).astype(jnp.bfloat16)
    grad_gate = (back_hidden * up_pre * slope).astype(jnp.bfloat16)
    token_grad = (
        lax.dot_general(
            grad_gate, full_gate, (((1,), (1,)), ((), ())), preferred_element_type=jnp.float32
        )
        + lax.dot_general(
            grad_up, full_up, (((1,), (1,)), ((), ())), preferred_element_type=jnp.float32
        )
    ).astype(jnp.bfloat16)
    gate_up = jnp.concatenate([grad_gate, grad_up], axis=1)
    token_cols, cot_cols = (
        lax.all_to_all(tokens, "node", split_axis=1, concat_axis=0, tiled=True),
        lax.all_to_all(cotangent, "node", split_axis=1, concat_axis=0, tiled=True),
    )
    piece_gu = lax.all_gather(gate_up, "node", axis=0, tiled=True)
    piece_hidden = lax.all_gather(hidden, "node", axis=0, tiled=True)
    summed = jnp.concatenate(
        [contract_rows(token_cols, piece_gu), contract_rows(cot_cols, piece_hidden)], axis=1
    )
    grad_scale = 1.0 / math.sqrt(tokens.shape[0] * node_count)
    merged = summed * grad_scale + error_memory[0].astype(jnp.float32)
    blocks = [merged[:, m * hidden_units : (m + 1) * hidden_units] for m in range(3)]
    row_terms = jnp.stack([jnp.dot(blocks[m], q_init[m], precision=highest) for m in range(3)])
    power_rows = lax.psum(row_terms.astype(jnp.bfloat16), "grp").astype(jnp.float32) / group_count
    local_gram = jnp.einsum("mdr,mds->mrs", power_rows, power_rows, precision=highest)
    gram_matrix = lax.psum(local_gram, "node")
    hats = []
    for m in range(3):
        factor = jnp.linalg.cholesky(gram_matrix[m])
        hats.append(jax.scipy.linalg.solve_triangular(factor, power_rows[m].T, lower=True).T)
    col_terms = jnp.stack([jnp.dot(blocks[m].T, hats[m], precision=highest) for m in range(3)])
    q_new = lax.psum(col_terms, ("node", "grp")) / group_count
    errors = [blocks[m] - jnp.dot(hats[m], q_new[m].T, precision=highest) for m in range(3)]
    new_error = jnp.concatenate(errors, axis=1).astype(jnp.bfloat16)[None]
    return (token_grad, new_error, jnp.stack(hats), q_new)


def solution(mesh):
    return jax.shard_map(
        on_device,
        mesh=mesh,
        in_specs=(
            P(("node", "grp"), None),
            P(("node", "grp"), None),
            P("node", None),
            P("node", None),
            P("node", None),
            P("grp", "node", None),
            P(),
        ),
        out_specs=(P(("node", "grp"), None), P("grp", "node", None), P(None, "node", None), P()),
        check_vma=False,
    )
```

profile of v0, /device:TPU:0, one launch (start us, length us, event | category | flops | bytes accessed | tf_op | source)
XLA Modules:
  0.0 512.1 jit_solution(15546751805123783097)
XLA Ops:
  9.4 37.6 %all-gather.6.cloned.1.call-done = bf16[1792,1024]{1,0:T(8,128)(2,1)} async-done(((bf16[224,1024]{1,0:T(8,128)(2,1)}), bf16[1792,1024]{1,0:T(8,128)(2,1)}) %all-gather.6.cloned.1.call-update) | async-done | bytes 3670032 | tf_op jit(solution)/shard_map/all_gather | solution.py:33
  47.0 5.2 %fusion.44 = f32[384,1024]{1,0:T(8,128)} fusion(bf16[384,1792]{1,0:T(8,128)(2,1)} %param.11, bf16[1792,1024]{1,0:T(8,128)(2,1)} %all-gather.6.cloned.1.call-done), kind=kOutput, calls=%fused_computation.92 | convolution fusion | flops 1409286144 | bytes 6619136 | tf_op jit(solution)/shard_map/dot_general | solution.py:39
  52.2 31.1 %all-gather.10.cloned.1.call-done = bf16[1792,1024]{1,0:T(8,128)(2,1)} async-done(((bf16[224,1024]{1,0:T(8,128)(2,1)}), bf16[1792,1024]{1,0:T(8,128)(2,1)}) %all-gather.10.cloned.1.call-update) | async-done | bytes 3670032 | tf_op jit(solution)/shard_map/all_gather | solution.py:31
  83.3 4.8 fusion.45
  88.1 31.5 %all-gather.8.cloned.1.call-done = bf16[1792,1024]{1,0:T(8,128)(2,1)} async-done(((bf16[224,1024]{1,0:T(8,128)(2,1)}), bf16[1792,1024]{1,0:T(8,128)(2,1)}) %all-gather.8.cloned.1.call-update) | async-done | bytes 3670032 | tf_op jit(solution)/shard_map/all_gather | solution.py:32
  119.6 6.4 %multiply_convert_fusion = (bf16[384,1024]{1,0:T(8,128)(2,1)}, bf16[384,1024]{1,0:T(8,128)(2,1)S(1)}, bf16[384,1024]{1,0:T(8,128)(2,1)S(1)}) fusion(f32[384,1024]{1,0:T(8,128)} %fusion.45, f32[384,1024]{1,0:T(8,128)} %fusion.44, bf16[384,1792]{1,0:T(8,128)(2,1)S(1)} %copy-done.2, bf16[1792,1024]{1,0:T(8,128)(2,1)} %all-gather.8.cloned.1.call-done), kind=kOutput, calls=%fused_computation.15 | convolution fusion | flops 1419116544 | bytes 10551296 | tf_op jit(solution)/shard_map/dot_general | solution.py:36
  126.9 1.4 pad_maximum_fusion
  128.3 1.3 copy-done.1
  129.6 1.5 copy.17
  131.1 3.6 all-to-all-start.1
  134.7 1.5 copy.15
  136.3 24.3 %all-to-all-done.1 = bf16[384,8,224]{0,2,1:T(8,128)(2,1)S(1)} async-done(((bf16[384,8,224]{0,2,1:T(8,128)(2,1)}), bf16[384,8,224]{0,2,1:T(8,128)(2,1)S(1)}, u32[]{:S(2)}, u32[]{:S(2)}) %all-to-all-start.1) | async-done | bytes 1376288 | tf_op jit(solution)/shard_map/all_to_all | solution.py:53
  160.5 3.6 all-to-all-start
  164.3 1.3 copy.25
  165.7 31.9 %all-to-all-done = bf16[384,8,224]{0,2,1:T(8,128)(2,1)S(1)} async-done(((bf16[384,8,224]{0,2,1:T(8,128)(2,1)}), bf16[384,8,224]{0,2,1:T(8,128)(2,1)S(1)}, u32[]{:S(2)}, u32[]{:S(2)}) %all-to-all-start) | async-done | bytes 1376288 | tf_op jit(solution)/shard_map/all_to_all | solution.py:52
  197.6 1.3 copy.24
  198.9 5.4 %fusion.46 = f32[384,1792]{1,0:T(8,128)} fusion(bf16[384,1024]{1,0:T(8,128)(2,1)S(1)} %copy-done.8, bf16[1792,1024]{1,0:T(8,128)(2,1)} %all-gather.10.cloned.1.call-done), kind=kOutput, calls=%fused_computation.94 | convolution fusion | flops 1409286144 | bytes 7208960 | tf_op jit(solution)/shard_map/dot_general | solution.py:43
  204.3 5.4 %convolution_bitcast_fusion.1 = f32[224,1024]{1,0:T(8,128)} fusion(bf16[3072,224]{0,1:T(8,128)(2,1)S(1)} %bitcast.133, bf16[3072,1024]{1,0:T(8,128)(2,1)} %all-gather.14.cloned.1.call-done), kind=kOutput, calls=%fused_computation.19 | convolution fusion | flops 1409286144 | bytes 8585216 | tf_op jit(solution)/shard_map/dot_general | solution.py:20
  209.7 64.7 %all-gather.12.cloned.1.call-done = bf16[3072,2048]{1,0:T(8,128)(2,1)} async-done(((bf16[384,2048]{1,0:T(8,128)(2,1)}), bf16[3072,2048]{1,0:T(8,128)(2,1)}) %all-gather.12.cloned.1.call-update) | async-done | bytes 12582928 | tf_op jit(solution)/shard_map/all_gather | solution.py:55
  274.4 6.4 %convolution_bitcast_fusion = f32[224,2048]{1,0:T(8,128)S(1)} fusion(bf16[3072,224]{0,1:T(8,128)(2,1)S(1)} %bitcast.134, bf16[3072,2048]{1,0:T(8,128)(2,1)} %all-gather.12.cloned.1.call-done), kind=kOutput, calls=%fused_computation.4 | convolution fusion | flops 2818572288 | bytes 15794176 | tf_op jit(solution)/shard_map/dot_general | solution.py:20
  285.2 20.5 %psum.21 = bf16[3,224,32]{1,2,0:T(8,128)(2,1)} all-reduce(bf16[3,224,32]{1,2,0:T(8,128)(2,1)} %pad_maximum_fusion.4), channel_id=1, replica_groups=mesh['node'=8,'grp'=4] {'grp'}, use_global_device_ids=true, to_apply=%region_0.0 | all-reduce | flops 21504 | bytes 86016 | tf_op jit(solution)/shard_map/psum | solution.py:64
  305.6 1.7 fusion.33
  307.4 1.4 convert_multiply_fusion
  308.8 24.0 %psum.22 = f32[3,32,32]{1,2,0:T(8,128)} all-reduce(f32[3,32,32]{1,2,0:T(8,128)} %fusion.33), channel_id=1, replica_groups=mesh['node'=8,'grp'=4] {'node'}, use_global_device_ids=true, to_apply=%region_1.0 | all-reduce | flops 3072 | bytes 24576 | tf_op jit(solution)/shard_map/psum | solution.py:66
  332.9 1.4 slice_bitcast_fusion.14
  335.0 1.4 copy.22
  336.4 1.4 copy.21
  337.8 1.4 fusion.39
  339.2 3.6 cholesky.59
  343.5 1.3 fusion.34
  344.8 3.8 custom-call.7
  348.5 3.6 cholesky.70
  352.9 1.3 fusion.35
  354.1 3.2 custom-call.8
  357.3 1.6 fusion.32
  358.9 1.6 fusion.31
  360.5 3.6 cholesky.81
  364.8 1.3 fusion.36
  366.0 3.2 custom-call.9
  369.2 1.0 fusion.30
  370.9 1.4 convolution_bitcast_fusion.3
  373.8 5.7 %fusion = bf16[384,1792]{1,0:T(8,128)(2,1)} fusion(f32[384,1792]{1,0:T(8,128)} %fusion.46, bf16[384,1024]{1,0:T(8,128)(2,1)S(1)} %get-tuple-element.8, bf16[1792,1024]{1,0:T(8,128)(2,1)} %all-gather.8.cloned.1.call-done), kind=kOutput, calls=%fused_computation.1 | convolution fusion | flops 1410662400 | bytes 8585216 | tf_op jit(solution)/shard_map/dot_general | solution.py:46
  380.2 119.2 %all-reduce.2.cloned.1.call-done = f32[3,1024,32]{1,2,0:T(8,128)} async-done(((f32[3,1024,32]{1,2,0:T(8,128)}), f32[3,1024,32]{1,2,0:T(8,128)}) %all-reduce.2.cloned.1.call-update) | async-done | bytes 393232 | tf_op jit(solution)/shard_map/psum | solution.py:72
  499.4 1.0 broadcast_multiply_fusion
  500.4 1.8 fusion.12
  502.2 0.9 fusion.13
  503.1 0.9 fusion.14
  504.1 1.2 pad_maximum_fusion.1
  (62 shorter events, 13.3 us)
Async XLA Ops:
  7.2 39.8 %all-gather.6.cloned.1.call-start = ((), (), s32[]{:S(2)}) async-start(), calls=%async_computation.2 | async-start | bytes 4128768 | tf_op jit(solution)/shard_map/all_gather | solution.py:33
  7.9 75.4 %all-gather.10.cloned.1.call-start = ((), (), s32[]{:S(2)}) async-start(), calls=%async_computation.4 | async-start | bytes 4128768 | tf_op jit(solution)/shard_map/all_gather | solution.py:31
  8.6 111.0 %all-gather.8.cloned.1.call-start = ((), (), s32[]{:S(2)}) async-start(), calls=%async_computation.3 | async-start | bytes 4128768 | tf_op jit(solution)/shard_map/all_gather | solution.py:32
  9.4 73.9 %copy-start.2 = (bf16[384,1792]{1,0:T(8,128)(2,1)S(1)}, bf16[384,1792]{1,0:T(8,128)(2,1)}, u32[]{:S(2)}) copy-start(bf16[384,1792]{1,0:T(8,128)(2,1)} %param.10) | copy-start | bytes 4128772
  9.4 194.9 %all-gather.14.cloned.1.call-start = ((), (), s32[]{:S(2)}) async-start(), calls=%async_computation.6 | async-start | bytes 7077888 | tf_op jit(solution)/shard_map/all_gather | solution.py:56
  126.0 0.9 copy-start.7
  126.0 148.4 %all-gather.12.cloned.1.call-start = ((), (), s32[]{:S(2)}) async-start(), calls=%async_computation.5 | async-start | bytes 14155776 | tf_op jit(solution)/shard_map/all_gather | solution.py:55
  128.2 1.3 copy-start.1
  131.1 29.4 %all-to-all-start.1 = ((bf16[384,8,224]{0,2,1:T(8,128)(2,1)}), bf16[384,8,224]{0,2,1:T(8,128)(2,1)S(1)}, u32[]{:S(2)}, u32[]{:S(2)}) async-start(bf16[384,8,224]{0,2,1:T(8,128)(2,1)} %bitcast.3), calls=%async_computation.1 | async-start | bytes 2752512 | tf_op jit(solution)/shard_map/all_to_all | solution.py:53
  160.5 37.1 %all-to-all-start = ((bf16[384,8,224]{0,2,1:T(8,128)(2,1)}), bf16[384,8,224]{0,2,1:T(8,128)(2,1)S(1)}, u32[]{:S(2)}, u32[]{:S(2)}) async-start(bf16[384,8,224]{0,2,1:T(8,128)(2,1)} %bitcast), calls=%async_computation | async-start | bytes 2752512 | tf_op jit(solution)/shard_map/all_to_all | solution.py:52
  164.1 335.3 %all-reduce.2.cloned.1.call-start = ((), (), s32[]{:S(2)}) async-start(), calls=%async_computation.7 | async-start | bytes 786432 | tf_op jit(solution)/shard_map/psum | solution.py:72
  197.6 1.3 copy-start.8
  198.9 5.4 %copy-start.4 = (bf16[8,28,8,384]{3,2,0,1:T(8,128)(2,1)S(1)}, bf16[8,28,8,384]{3,2,0,1:T(8,128)(2,1)}, u32[]{:S(2)}) copy-start(bf16[8,28,8,384]{3,2,0,1:T(8,128)(2,1)} %copy.25) | copy-start | bytes 4128772
  204.3 70.1 %copy-start.5 = (bf16[8,28,8,384]{3,2,0,1:T(8,128)(2,1)S(1)}, bf16[8,28,8,384]{3,2,0,1:T(8,128)(2,1)}, u32[]{:S(2)}) copy-start(bf16[8,28,8,384]{3,2,0,1:T(8,128)(2,1)} %copy.24) | copy-start | bytes 4128772
  274.4 6.4 %copy-start.3 = (bf16[1,224,3072]{2,1,0:T(8,128)(2,1)S(1)}, bf16[1,224,3072]{2,1,0:T(8,128)(2,1)}, u32[]{:S(2)}) copy-start(bf16[1,224,3072]{2,1,0:T(8,128)(2,1)} %param.15) | copy-start | bytes 4128772
  274.4 6.4 %copy-start.6 = (f32[224,1024]{1,0:T(8,128)S(1)}, f32[224,1024]{1,0:T(8,128)}, u32[]{:S(2)}) copy-start(f32[224,1024]{1,0:T(8,128)} %convolution_bitcast_fusion.1) | copy-start | bytes 2752516
  280.8 1.0 copy-start.16
  369.2 3.1 copy-start.9
  370.2 2.8 copy-start.14
  373.8 5.7 %copy-start.10 = (f32[32,224]{1,0:T(8,128)S(1)}, f32[32,224]{1,0:T(8,128)}, u32[]{:S(2)}) copy-start(f32[32,224]{1,0:T(8,128)} %fusion.32) | copy-start | bytes 86020
  373.8 5.7 %copy-start.12 = (f32[32,224]{1,0:T(8,128)S(1)}, f32[32,224]{1,0:T(8,128)}, u32[]{:S(2)}) copy-start(f32[32,224]{1,0:T(8,128)} %fusion.31) | copy-start | bytes 86020
  373.8 5.7 %copy-start.15 = (f32[32,224]{1,0:T(8,128)S(1)}, f32[32,224]{1,0:T(8,128)}, u32[]{:S(2)}) copy-start(f32[32,224]{1,0:T(8,128)} %copy-done.14) | copy-start | bytes 86020
  379.5 122.7 %copy-start.13 = (f32[32,224]{1,0:T(8,128)S(1)}, f32[32,224]{1,0:T(8,128)}, u32[]{:S(2)}) copy-start(f32[32,224]{1,0:T(8,128)} %fusion.31) | copy-start | bytes 86020
  500.4 3.7 copy-start
  500.4 2.7 copy-start.11
Sparse Core Ops, SparseCore 0:
  9.9 37.0 all-gather.5
  48.9 34.3 all-gather.9
  85.2 34.3 all-gather.7
  126.1 74.4 all-gather.13
  202.4 71.9 all-gather.11
  373.9 125.4 all-reduce.1
where the time goes:
time: 514 us; the launch traced here: 512 us
  waiting for transfers between devices  342 us (67%)
  matrix products  54.2 us (11%)
  blocking collectives  44.5 us (9%)
  other arithmetic  35.7 us (7%)
  between operations  14.4 us (3%)
  local copies, waits for them, and re-layouts  13.4 us (3%)
  starting transfers between devices  7.6 us (1%)
    psum x1, waiting for transfers between devices, on_device(): q_new = lax.psum(col_terms, ('node', 'grp')) / group_count  119 us
    all_gather x1, waiting for transfers between devices, on_device(): piece_gu = lax.all_gather(gate_up, 'node', axis=0, tiled=True)  64.7 us
    all_gather x1, waiting for transfers between devices, on_device(): lax.all_gather(down_weight_t, 'node', axis=0, tiled=True)  37.6 us
    all_to_all x1, waiting for transfers between devices, on_device(): lax.all_to_all(tokens, 'node', split_axis=1, concat_axis=0, tiled=True)  31.9 us
    all_gather x1, waiting for transfers between devices, on_device(): lax.all_gather(up_weight, 'node', axis=0, tiled=True)  31.5 us
    all_gather x1, waiting for transfers between devices, on_device(): lax.all_gather(gate_weight, 'node', axis=0, tiled=True)  31.1 us
    all_to_all x1, waiting for transfers between devices, on_device(): lax.all_to_all(cotangent, 'node', split_axis=1, concat_axis=0, tiled=True)  24.3 us
    psum x1, blocking collectives, on_device(): gram_matrix = lax.psum(local_gram, 'node')  24 us
  transfers between devices with their start and end apart: 8, of which 7 were waited for; matrix products, arithmetic and copies ran while one was open for 7% of the time, Pallas kernels for 0%

commit v1 on v0

--- a/solution.py
+++ b/solution.py
@@ -69,7 +69,7 @@
         factor = jnp.linalg.cholesky(gram_matrix[m])
         hats.append(jax.scipy.linalg.solve_triangular(factor, power_rows[m].T, lower=True).T)
     col_terms = jnp.stack([jnp.dot(blocks[m].T, hats[m], precision=highest) for m in range(3)])
-    q_new = lax.psum(col_terms, ("node", "grp")) / group_count
+    q_new = lax.psum(lax.psum(col_terms, "grp"), "node") / group_count
     errors = [blocks[m] - jnp.dot(hats[m], q_new[m].T, precision=highest) for m in range(3)]
     new_error = jnp.concatenate(errors, axis=1).astype(jnp.bfloat16)[None]
     return (token_grad, new_error, jnp.stack(hats), q_new)

time: 514 us -> 479 us (0.932)
  waiting for transfers between devices: 342 us -> 308 us
    psum x1 -> x2, waiting for transfers between devices: 119 us -> 79.2 us  [on_device(): q_new = lax.psum(lax.psum(col_terms, 'grp'), 'node') / group_count]
  transfers between devices with their start and end apart: 8 -> 9, of which waited for: 7 -> 9; matrix products, arithmetic and copies ran while one was open for 7% -> 7% of each run, Pallas kernels for 0% -> 0%
where the time goes in v1:
time: 479 us; the launch traced here: 478 us
  waiting for transfers between devices  308 us (64%)
  matrix products  54.2 us (11%)
  blocking collectives  44.5 us (9%)
  other arithmetic  35.6 us (7%)
  between operations  14.4 us (3%)
  local copies, waits for them, and re-layouts  13.4 us (3%)
  starting transfers between devices  7.46 us (2%)
    psum x2, waiting for transfers between devices, on_device(): q_new = lax.psum(lax.psum(col_terms, 'grp'), 'node') / group_count  79.2 us
    all_gather x1, waiting for transfers between devices, on_device(): piece_gu = lax.all_gather(gate_up, 'node', axis=0, tiled=True)  68.4 us
    all_gather x1, waiting for transfers between devices, on_device(): lax.all_gather(down_weight_t, 'node', axis=0, tiled=True)  37.6 us
    all_to_all x1, waiting for transfers between devices, on_device(): lax.all_to_all(tokens, 'node', split_axis=1, concat_axis=0, tiled=True)  32.1 us
    all_gather x1, waiting for transfers between devices, on_device(): lax.all_gather(up_weight, 'node', axis=0, tiled=True)  31.5 us
    all_gather x1, waiting for transfers between devices, on_device(): lax.all_gather(gate_weight, 'node', axis=0, tiled=True)  31.1 us
    all_to_all x1, waiting for transfers between devices, on_device(): lax.all_to_all(cotangent, 'node', split_axis=1, concat_axis=0, tiled=True)  24.4 us
    psum x1, blocking collectives, on_device(): gram_matrix = lax.psum(local_gram, 'node')  24 us
  transfers between devices with their start and end apart: 9, of which 9 were waited for; matrix products, arithmetic and copies ran while one was open for 7% of the time, Pallas kernels for 0%

profile of v1, /device:TPU:0, one launch (start us, length us, event | category | flops | bytes accessed | tf_op | source)
XLA Modules:
  0.0 477.6 jit_solution(10039222422016746186)
XLA Ops:
  9.4 37.6 %all-gather.6.cloned.1.call-done = bf16[1792,1024]{1,0:T(8,128)(2,1)} async-done(((bf16[224,1024]{1,0:T(8,128)(2,1)}), bf16[1792,1024]{1,0:T(8,128)(2,1)}) %all-gather.6.cloned.1.call-update) | async-done | bytes 3670032 | tf_op jit(solution)/shard_map/all_gather | solution.py:33
  47.0 5.2 %fusion.44 = f32[384,1024]{1,0:T(8,128)} fusion(bf16[384,1792]{1,0:T(8,128)(2,1)} %param.11, bf16[1792,1024]{1,0:T(8,128)(2,1)} %all-gather.6.cloned.1.call-done), kind=kOutput, calls=%fused_computation.92 | convolution fusion | flops 1409286144 | bytes 6619136 | tf_op jit(solution)/shard_map/dot_general | solution.py:39
  52.2 31.1 %all-gather.10.cloned.1.call-done = bf16[1792,1024]{1,0:T(8,128)(2,1)} async-done(((bf16[224,1024]{1,0:T(8,128)(2,1)}), bf16[1792,1024]{1,0:T(8,128)(2,1)}) %all-gather.10.cloned.1.call-update) | async-done | bytes 3670032 | tf_op jit(solution)/shard_map/all_gather | solution.py:31
  83.3 4.8 %fusion.45 = f32[384,1024]{1,0:T(8,128)} fusion(bf16[384,1792]{1,0:T(8,128)(2,1)S(1)} %copy-done.2, bf16[1792,1024]{1,0:T(8,128)(2,1)} %all-gather.10.cloned.1.call-done), kind=kOutput, calls=%fused_computation.93 | convolution fusion | flops 1409286144 | bytes 6619136 | tf_op jit(solution)/shard_map/dot_general | solution.py:35
  88.1 31.5 %all-gather.8.cloned.1.call-done = bf16[1792,1024]{1,0:T(8,128)(2,1)} async-done(((bf16[224,1024]{1,0:T(8,128)(2,1)}), bf16[1792,1024]{1,0:T(8,128)(2,1)}) %all-gather.8.cloned.1.call-update) | async-done | bytes 3670032 | tf_op jit(solution)/shard_map/all_gather | solution.py:32
  119.6 6.4 %multiply_convert_fusion = (bf16[384,1024]{1,0:T(8,128)(2,1)}, bf16[384,1024]{1,0:T(8,128)(2,1)S(1)}, bf16[384,1024]{1,0:T(8,128)(2,1)S(1)}) fusion(f32[384,1024]{1,0:T(8,128)} %fusion.45, f32[384,1024]{1,0:T(8,128)} %fusion.44, bf16[384,1792]{1,0:T(8,128)(2,1)S(1)} %copy-done.2, bf16[1792,1024]{1,0:T(8,128)(2,1)} %all-gather.8.cloned.1.call-done), kind=kOutput, calls=%fused_computation.15 | convolution fusion | flops 1419116544 | bytes 10551296 | tf_op jit(solution)/shard_map/dot_general | solution.py:36
  126.9 1.3 pad_maximum_fusion
  128.2 1.3 copy-done.1
  129.5 1.5 copy.17
  131.0 3.6 all-to-all-start.1
  134.6 1.5 copy.15
  136.2 24.4 %all-to-all-done.1 = bf16[384,8,224]{0,2,1:T(8,128)(2,1)S(1)} async-done(((bf16[384,8,224]{0,2,1:T(8,128)(2,1)}), bf16[384,8,224]{0,2,1:T(8,128)(2,1)S(1)}, u32[]{:S(2)}, u32[]{:S(2)}) %all-to-all-start.1) | async-done | bytes 1376288 | tf_op jit(solution)/shard_map/all_to_all | solution.py:53
  160.5 3.6 all-to-all-start
  164.2 1.3 copy.25
  165.5 32.1 %all-to-all-done = bf16[384,8,224]{0,2,1:T(8,128)(2,1)S(1)} async-done(((bf16[384,8,224]{0,2,1:T(8,128)(2,1)}), bf16[384,8,224]{0,2,1:T(8,128)(2,1)S(1)}, u32[]{:S(2)}, u32[]{:S(2)}) %all-to-all-start) | async-done | bytes 1376288 | tf_op jit(solution)/shard_map/all_to_all | solution.py:52
  197.6 1.3 copy.24
  198.9 1.8 all-gather.14.cloned.1.call-done
  200.7 5.4 %convolution_bitcast_fusion.1 = f32[224,1024]{1,0:T(8,128)} fusion(bf16[3072,224]{0,1:T(8,128)(2,1)S(1)} %bitcast.133, bf16[3072,1024]{1,0:T(8,128)(2,1)} %all-gather.14.cloned.1.call-done), kind=kOutput, calls=%fused_computation.19 | convolution fusion | flops 1409286144 | bytes 8585216 | tf_op jit(solution)/shard_map/dot_general | solution.py:20
  206.1 68.4 %all-gather.12.cloned.1.call-done = bf16[3072,2048]{1,0:T(8,128)(2,1)} async-done(((bf16[384,2048]{1,0:T(8,128)(2,1)}), bf16[3072,2048]{1,0:T(8,128)(2,1)}) %all-gather.12.cloned.1.call-update) | async-done | bytes 12582928 | tf_op jit(solution)/shard_map/all_gather | solution.py:55
  274.4 6.4 %convolution_bitcast_fusion = f32[224,2048]{1,0:T(8,128)S(1)} fusion(bf16[3072,224]{0,1:T(8,128)(2,1)S(1)} %bitcast.134, bf16[3072,2048]{1,0:T(8,128)(2,1)} %all-gather.12.cloned.1.call-done), kind=kOutput, calls=%fused_computation.4 | convolution fusion | flops 2818572288 | bytes 15794176 | tf_op jit(solution)/shard_map/dot_general | solution.py:20
  285.2 20.5 %psum.28 = bf16[3,224,32]{1,2,0:T(8,128)(2,1)} all-reduce(bf16[3,224,32]{1,2,0:T(8,128)(2,1)} %pad_maximum_fusion.4), channel_id=1, replica_groups=mesh['node'=8,'grp'=4] {'grp'}, use_global_device_ids=true, to_apply=%region_0.0 | all-reduce | flops 21504 | bytes 86016 | tf_op jit(solution)/shard_map/psum | solution.py:64
  305.6 1.7 fusion.33
  307.4 1.4 convert_multiply_fusion
  308.8 24.0 %psum.29 = f32[3,32,32]{1,2,0:T(8,128)} all-reduce(f32[3,32,32]{1,2,0:T(8,128)} %fusion.33), channel_id=1, replica_groups=mesh['node'=8,'grp'=4] {'node'}, use_global_device_ids=true, to_apply=%region_1.0 | all-reduce | flops 3072 | bytes 24576 | tf_op jit(solution)/shard_map/psum | solution.py:66
  332.8 1.4 slice_bitcast_fusion.14
  335.0 1.4 copy.22
  336.4 1.4 copy.21
  337.8 1.4 fusion.39
  339.2 3.6 cholesky.59
  343.5 1.3 fusion.34
  344.7 3.8 custom-call.7
  348.5 3.6 cholesky.70
  352.8 1.3 fusion.35
  354.1 3.2 custom-call.8
  357.2 1.6 fusion.32
  358.9 1.6 fusion.31
  360.4 3.6 cholesky.81
  364.7 1.3 fusion.36
  366.0 3.2 custom-call.9
  369.1 1.0 fusion.30
  370.9 1.4 convolution_bitcast_fusion.3
  373.8 5.5 %fusion.46 = f32[384,1792]{1,0:T(8,128)} fusion(bf16[384,1024]{1,0:T(8,128)(2,1)} %copy-done.7, bf16[1792,1024]{1,0:T(8,128)(2,1)} %all-gather.10.cloned.1.call-done), kind=kOutput, calls=%fused_computation.94 | convolution fusion | flops 1409286144 | bytes 7208960 | tf_op jit(solution)/shard_map/dot_general | solution.py:43
  379.3 28.3 %all-reduce.3.cloned.1.call-done = f32[3,1024,32]{1,2,0:T(8,128)} async-done(((f32[3,1024,32]{1,2,0:T(8,128)}), f32[3,1024,32]{1,2,0:T(8,128)}) %all-reduce.3.cloned.1.call-update) | async-done | bytes 393232 | tf_op jit(solution)/shard_map/psum | solution.py:72
  407.7 5.6 %fusion = bf16[384,1792]{1,0:T(8,128)(2,1)} fusion(f32[384,1792]{1,0:T(8,128)} %fusion.46, bf16[384,1024]{1,0:T(8,128)(2,1)S(1)} %get-tuple-element.8, bf16[1792,1024]{1,0:T(8,128)(2,1)} %all-gather.8.cloned.1.call-done), kind=kOutput, calls=%fused_computation.1 | convolution fusion | flops 1410662400 | bytes 8585216 | tf_op jit(solution)/shard_map/dot_general | solution.py:46
  414.0 50.9 %all-reduce.5.cloned.1.call-done = f32[3,1024,32]{1,2,0:T(8,128)} async-done(((f32[3,1024,32]{1,2,0:T(8,128)}), f32[3,1024,32]{1,2,0:T(8,128)}) %all-reduce.5.cloned.1.call-update) | async-done | bytes 393232 | tf_op jit(solution)/shard_map/psum | solution.py:72
  464.8 1.0 broadcast_multiply_fusion
  465.9 1.8 fusion.12
  469.6 1.2 pad_maximum_fusion.1
  (63 shorter events, 15.0 us)
Async XLA Ops:
  7.2 39.8 %all-gather.6.cloned.1.call-start = ((), (), s32[]{:S(2)}) async-start(), calls=%async_computation.2 | async-start | bytes 4128768 | tf_op jit(solution)/shard_map/all_gather | solution.py:33
  7.9 75.4 %all-gather.10.cloned.1.call-start = ((), (), s32[]{:S(2)}) async-start(), calls=%async_computation.4 | async-start | bytes 4128768 | tf_op jit(solution)/shard_map/all_gather | solution.py:31
  8.6 111.0 %all-gather.8.cloned.1.call-start = ((), (), s32[]{:S(2)}) async-start(), calls=%async_computation.3 | async-start | bytes 4128768 | tf_op jit(solution)/shard_map/all_gather | solution.py:32
  9.4 73.9 %copy-start.2 = (bf16[384,1792]{1,0:T(8,128)(2,1)S(1)}, bf16[384,1792]{1,0:T(8,128)(2,1)}, u32[]{:S(2)}) copy-start(bf16[384,1792]{1,0:T(8,128)(2,1)} %param.10) | copy-start | bytes 4128772
  9.4 191.3 %all-gather.14.cloned.1.call-start = ((), (), s32[]{:S(2)}) async-start(), calls=%async_computation.6 | async-start | bytes 7077888 | tf_op jit(solution)/shard_map/all_gather | solution.py:56
  126.0 0.9 copy-start.7
  126.0 148.4 %all-gather.12.cloned.1.call-start = ((), (), s32[]{:S(2)}) async-start(), calls=%async_computation.5 | async-start | bytes 14155776 | tf_op jit(solution)/shard_map/all_gather | solution.py:55
  128.1 1.3 copy-start.1
  131.0 29.5 %all-to-all-start.1 = ((bf16[384,8,224]{0,2,1:T(8,128)(2,1)}), bf16[384,8,224]{0,2,1:T(8,128)(2,1)S(1)}, u32[]{:S(2)}, u32[]{:S(2)}) async-start(bf16[384,8,224]{0,2,1:T(8,128)(2,1)} %bitcast.3), calls=%async_computation.1 | async-start | bytes 2752512 | tf_op jit(solution)/shard_map/all_to_all | solution.py:53
  160.5 37.1 %all-to-all-start = ((bf16[384,8,224]{0,2,1:T(8,128)(2,1)}), bf16[384,8,224]{0,2,1:T(8,128)(2,1)S(1)}, u32[]{:S(2)}, u32[]{:S(2)}) async-start(bf16[384,8,224]{0,2,1:T(8,128)(2,1)} %bitcast), calls=%async_computation | async-start | bytes 2752512 | tf_op jit(solution)/shard_map/all_to_all | solution.py:52
  164.1 243.5 %all-reduce.3.cloned.1.call-start = ((), (), s32[]{:S(2)}) async-start(), calls=%async_computation.7 | async-start | bytes 786432 | tf_op jit(solution)/shard_map/psum | solution.py:72
  165.5 35.2 %copy-start.4 = (bf16[8,28,8,384]{3,2,0,1:T(8,128)(2,1)S(1)}, bf16[8,28,8,384]{3,2,0,1:T(8,128)(2,1)}, u32[]{:S(2)}) copy-start(bf16[8,28,8,384]{3,2,0,1:T(8,128)(2,1)} %copy.25) | copy-start | bytes 4128772
  200.7 73.8 %copy-start.5 = (bf16[8,28,8,384]{3,2,0,1:T(8,128)(2,1)S(1)}, bf16[8,28,8,384]{3,2,0,1:T(8,128)(2,1)}, u32[]{:S(2)}) copy-start(bf16[8,28,8,384]{3,2,0,1:T(8,128)(2,1)} %copy.24) | copy-start | bytes 4128772
  274.4 6.4 %copy-start.3 = (bf16[1,224,3072]{2,1,0:T(8,128)(2,1)S(1)}, bf16[1,224,3072]{2,1,0:T(8,128)(2,1)}, u32[]{:S(2)}) copy-start(bf16[1,224,3072]{2,1,0:T(8,128)(2,1)} %param.15) | copy-start | bytes 4128772
  274.4 6.4 %copy-start.6 = (f32[224,1024]{1,0:T(8,128)S(1)}, f32[224,1024]{1,0:T(8,128)}, u32[]{:S(2)}) copy-start(f32[224,1024]{1,0:T(8,128)} %convolution_bitcast_fusion.1) | copy-start | bytes 2752516
  280.8 1.0 copy-start.15
  369.1 3.1 copy-start.8
  370.2 2.8 copy-start.13
  373.8 91.1 %all-reduce.5.cloned.1.call-start = ((), (), s32[]{:S(2)}) async-start(), calls=%async_computation.8 | async-start | bytes 786432 | tf_op jit(solution)/shard_map/psum | solution.py:72
  407.7 5.7 %copy-start.9 = (f32[32,224]{1,0:T(8,128)S(1)}, f32[32,224]{1,0:T(8,128)}, u32[]{:S(2)}) copy-start(f32[32,224]{1,0:T(8,128)} %fusion.32) | copy-start | bytes 86020
  407.7 5.6 %copy-start.11 = (f32[32,224]{1,0:T(8,128)S(1)}, f32[32,224]{1,0:T(8,128)}, u32[]{:S(2)}) copy-start(f32[32,224]{1,0:T(8,128)} %fusion.31) | copy-start | bytes 86020
  407.7 5.6 %copy-start.14 = (f32[32,224]{1,0:T(8,128)S(1)}, f32[32,224]{1,0:T(8,128)}, u32[]{:S(2)}) copy-start(f32[32,224]{1,0:T(8,128)} %copy-done.13) | copy-start | bytes 86020
  413.3 54.4 %copy-start.12 = (f32[32,224]{1,0:T(8,128)S(1)}, f32[32,224]{1,0:T(8,128)}, u32[]{:S(2)}) copy-start(f32[32,224]{1,0:T(8,128)} %fusion.31) | copy-start | bytes 86020
  465.9 3.7 copy-start
  465.9 2.7 copy-start.10
Sparse Core Ops, SparseCore 0:
  9.9 37.0 all-gather.5
  48.9 34.3 all-gather.9
  85.2 34.3 all-gather.7
  126.1 74.4 all-gather.13
  202.4 71.9 all-gather.11
  373.9 33.6 all-reduce.2
  410.7 54.1 all-reduce.4
